TPU v7x, 32 devices: a whole 2x2x4 slice. The times are simulated.
32 devices in a mesh: row: 8 (over z, x), col: 4 (over y, core).
Axes of the slice: x: 2, y: 2, z: 4, core: 2. Of those that a mesh axis runs over, the one named last changes fastest.
Arguments:
- density_first: bfloat16 [12288, 12288], P('row', 'col'), may hold values from -0.0068359375 to 0.0068359375
- density_second: bfloat16 [12288, 12288], P('row', 'col'), may hold values from -0.0068359375 to 0.0068359375
- basis: bfloat16 [64, 4096, 896], P(('row', 'col')), may hold values from -6 to 6
- tile_list: int32 [64, 7], P(('row', 'col')), may hold values from 0 to 95, as said below
- tile_count: int32 [64], P(('row', 'col')), may hold values from 5 to 7, as said below
- point_count: int32 [64], P(('row', 'col')), may hold values from 1024 to 4096, as said below
- offsets: float32 [3, 64, 4096], P(None, ('row', 'col')), may hold values from -5 to 5
- weights: float32 [64, 4096], P(('row', 'col')), may hold values from 0.05 to 1
- atom_of_point: int32 [64, 4096], P(('row', 'col')), may hold values from 0 to 1023, as said below
Outputs:
- density: float32 [2, 64, 4096], P(None, ('row', 'col'))
- moments: float32 [2, 9, 1024], replicated
Inputs may be any that keep to these rules, and one draw needn't show every extreme that they name: `tile_list`: the 7 tile numbers of each batch are 7 consecutive numbers in some order. `tile_count`: some batch has 7. `point_count`: some batch has 4096. `atom_of_point`: the points of batch g belong to atoms (g * 16 + j) mod 1024 with j from 0 to 7.
All inputs are finite; a program needn't handle non-finite values.
Results may differ from a plain program's by a relative error of at most 0.0003.
Values may be sent and summed in bfloat16 or wider, within the bound.
A program may use at most 192 MiB of HBM per device.

v0:
```python
import jax
import jax.numpy as jnp
from jax import lax
from jax.sharding import PartitionSpec as P

TILE = 128
ATOMS = 1024


def harmonics(offsets):
    first_axis = offsets[0]
    second_axis = offsets[1]
    third_axis = offsets[2]
    radius_sq = first_axis * first_axis + second_axis * second_axis + third_axis * third_axis
    return jnp.stack(
        [
            jnp.ones_like(first_axis),
            first_axis,
            second_axis,
            third_axis,
            first_axis * second_axis,
            second_axis * third_axis,
            3.0 * third_axis * third_axis - radius_sq,
            first_axis * third_axis,
            first_axis * first_axis - second_axis * second_axis,
        ]
    )


def local(
    density_first,
    density_second,
    basis,
    tile_list,
    tile_count,
    point_count,
    offsets,
    weights,
    atom_of_point,
):
    row_count = lax.axis_size("row")
    col_count = lax.axis_size("col")
    tile_size = TILE
    local_rows = density_first.shape[0] // tile_size
    local_cols = density_first.shape[1] // tile_size
    batches_dev = tile_list.shape[0]
    run_length = tile_list.shape[1]
    points = basis.shape[1]
    row_slots = -(-run_length // row_count)
    col_slots = -(-run_length // col_count)
    my_row = lax.axis_index("row")
    my_col = lax.axis_index("col")
    own_start = jnp.min(tile_list, axis=1)
    starts = lax.all_gather(own_start, ("row", "col"), axis=0, tiled=True)
    run_end = starts[:, None] + run_length
    first_row = starts + (my_row - starts) % row_count
    row_tile = first_row[:, None] + row_count * jnp.arange(row_slots, dtype=jnp.int32)[None, :]
    row_ok = row_tile < run_end
    row_local = jnp.where(row_ok, row_tile // row_count, 0)
    first_col = starts + (my_col - starts) % col_count
    col_tile = first_col[:, None] + col_count * jnp.arange(col_slots, dtype=jnp.int32)[None, :]
    col_ok = col_tile < run_end
    col_local = jnp.where(col_ok, col_tile // col_count, 0)
    wanted = row_ok[:, :, None] & col_ok[:, None, :]

    def pack_tiles(stored):
        tile_grid = stored.reshape(local_rows, tile_size, local_cols, tile_size).transpose(
            0, 2, 1, 3
        )
        picked = tile_grid[row_local[:, :, None], col_local[:, None, :]]
        picked = jnp.where(wanted[..., None, None], picked, jnp.zeros((), stored.dtype))
        return picked.reshape(
            row_count, col_count, batches_dev, row_slots, col_slots, tile_size, tile_size
        )

    outgoing_first = pack_tiles(density_first)
    outgoing_second = pack_tiles(density_second)
    flat_shape = (row_count * col_count,) + outgoing_first.shape[2:]
    flat_first = outgoing_first.reshape(flat_shape)
    flat_second = outgoing_second.reshape(flat_shape)
    moved_first, moved_second = (
        lax.all_to_all(flat_first, ("row", "col"), split_axis=0, concat_axis=0, tiled=True),
        lax.all_to_all(flat_second, ("row", "col"), split_axis=0, concat_axis=0, tiled=True),
    )
    arrived_first = moved_first.reshape(outgoing_first.shape)
    arrived_second = moved_second.reshape(outgoing_second.shape)
    offset_in_run = tile_list - own_start[:, None]
    owner_row = tile_list % row_count
    slot_row = offset_in_run // row_count
    owner_col = tile_list % col_count
    slot_col = offset_in_run // col_count
    batch_ids = jnp.arange(batches_dev, dtype=jnp.int32)[:, None, None]

    def assemble(arrived):
        blocks = arrived[
            owner_row[:, :, None],
            owner_col[:, None, :],
            batch_ids,
            slot_row[:, :, None],
            slot_col[:, None, :],
        ]
        return blocks.transpose(0, 1, 3, 2, 4).reshape(
            batches_dev, run_length * tile_size, run_length * tile_size
        )

    col_mask = jnp.arange(run_length)[None, :] < tile_count[:, None]
    col_mask = jnp.repeat(col_mask, tile_size, axis=1).astype(jnp.bfloat16)
    masked = basis * col_mask[:, None, :]
    point_mask = (jnp.arange(points)[None, :] < point_count[:, None]).astype(jnp.float32)

    def density_of(arrived):
        block = assemble(arrived)
        product = jnp.einsum("bpi,bij->bpj", masked, block, preferred_element_type=jnp.float32)
        return jnp.sum(product * masked.astype(jnp.float32), axis=2) * point_mask

    density = jnp.stack([density_of(arrived_first), density_of(arrived_second)])
    harmonic = harmonics(offsets)
    moment_terms = density[:, None] * (weights[None, None] * harmonic[None])
    flat_terms = moment_terms.reshape(2 * 9, -1)
    one_hot = (
        atom_of_point.reshape(-1)[:, None] == jnp.arange(ATOMS, dtype=jnp.int32)[None, :]
    ).astype(jnp.float32)
    partial_value = jnp.dot(
        flat_terms, one_hot, precision=lax.Precision.HIGHEST, preferred_element_type=jnp.float32
    )
    moments = lax.psum(partial_value, ("row", "col"))
    return (density, moments.reshape(2, 9, ATOMS))


def solution(mesh):
    placed = (
        P("row", "col"),
        P("row", "col"),
        P(("row", "col"), None, None),
        P(("row", "col"), None),
        P(("row", "col")),
        P(("row", "col")),
        P(None, ("row", "col"), None),
        P(("row", "col"), None),
        P(("row", "col"), None),
    )
    return jax.shard_map(
        local,
        mesh=mesh,
        in_specs=placed,
        out_specs=(P(None, ("row", "col"), None), P()),
        check_vma=False,
    )
```

profile of v0, /device:TPU:0, one launch (start us, length us, event | category | flops | bytes accessed | tf_op | source)
XLA Modules:
  0.0 516.1 jit_solution(7729851914212681637)
XLA Ops:
  7.2 0.8 fusion.11
  8.0 0.2 dynamic-update-slice
  8.2 42.0 %all-reduce = s32[64]{0:T(128)S(1)} all-reduce(s32[64]{0:T(128)S(1)} %dynamic-update-slice), channel_id=1, replica_groups=mesh['row'=8,'col'=4] {'row','col'}, use_global_device_ids=true, to_apply=%add | all-reduce | flops 64 | bytes 512
  50.2 0.1 add.135
  50.4 0.1 lt.139
  50.5 0.1 compare_select_fusion
  50.6 0.1 copy.49
  50.7 0.1 reshape.452
  50.8 9.8 %copy.68 = bf16[192,8,24,128]{3,2,1,0:T(8,128)(2,1)} copy(bf16[192,8,24,128]{3,1,2,0:T(8,128)(2,1)} %bitcast.60) | data formatting | bytes 18874368
  60.6 10.0 %copy.75 = bf16[12,128,24,128]{3,1,2,0:T(8,128)(2,1)} copy(bf16[12,128,24,128]{3,2,1,0:T(8,128)(2,1)} %bitcast.51) | data formatting | bytes 18874368 | tf_op jit(solution)/shard_map/reshape | solution.py:67
  70.6 9.9 %copy.67 = bf16[192,8,24,128]{3,2,1,0:T(8,128)(2,1)} copy(bf16[192,8,24,128]{3,1,2,0:T(8,128)(2,1)} %bitcast.61) | data formatting | bytes 18874368
  80.5 10.1 %copy.76 = bf16[12,128,24,128]{3,1,2,0:T(8,128)(2,1)} copy(bf16[12,128,24,128]{3,2,1,0:T(8,128)(2,1)} %bitcast.52) | data formatting | bytes 18874368 | tf_op jit(solution)/shard_map/reshape | solution.py:67
  90.6 6.8 %gather_fusion.2 = bf16[128,128,128]{2,1,0:T(8,128)(2,1)} fusion(bf16[12,24,128,128]{3,2,1,0:T(8,128)(2,1)} %bitcast.53, s32[128]{0:T(128)S(1)} %reshape.452), kind=kCustom, calls=%fused_computation.2 | custom fusion | bytes 8389632 | tf_op jit(solution)/shard_map/gather | solution.py:70
  97.4 6.7 %gather_fusion = bf16[128,128,128]{2,1,0:T(8,128)(2,1)} fusion(bf16[12,24,128,128]{3,2,1,0:T(8,128)(2,1)} %bitcast.54, s32[128]{0:T(128)S(1)} %reshape.452), kind=kCustom, calls=%fused_computation | custom fusion | bytes 8389632 | tf_op jit(solution)/shard_map/gather | solution.py:70
  104.2 0.1 and.74
  104.3 0.2 compare_and_fusion
  104.5 5.2 broadcast_select_fusion.1
  109.6 97.9 %all_to_all.10 = bf16[32,2,1,2,128,128]{5,4,3,1,2,0:T(8,128)(2,1)} all-to-all(bf16[32,2,1,2,128,128]{5,4,3,1,2,0:T(8,128)(2,1)S(1)} %get-tuple-element.13), channel_id=1, replica_groups=mesh['row'=8,'col'=4] {'row','col'}, dimensions={0} | all-to-all | bytes 8388608 | tf_op jit(solution)/shard_map/all_to_all | solution.py:83
  207.5 0.0 copy-start.5
  207.5 3.8 all-to-all-start
  211.3 0.5 all-reduce.3.cloned.1.call-start
  211.9 0.0 copy-done.5
  211.9 0.1 fusion.15
  212.0 0.1 or_or_fusion
  212.0 0.1 reshape.458
  212.1 0.0 copy-start.7
  212.1 0.0 copy-start.4
  212.1 0.0 copy-start.1
  212.2 0.0 copy-start.3
  212.2 19.9 %copy.46 = bf16[2,4096,896]{1,2,0:T(8,128)(2,1)} copy(bf16[2,4096,896]{2,1,0:T(8,128)(2,1)} %param.11) | data formatting | bytes 29360128 | tf_op args[2]
  232.1 0.0 copy-done.7
  232.1 0.1 compare_convert_fusion
  232.2 0.1 broadcast_bitcast_fusion
  232.2 0.0 copy-done.4
  232.3 0.0 copy-done.1
  232.4 0.1 fusion.9
  232.5 0.0 copy-done.3
  232.5 0.1 broadcast_multiply_fusion.1
  232.6 4.2 gather_fusion.3
  236.9 4.5 copy.56
  241.4 7.4 %reshape.487 = bf16[2,896,896]{2,1,0:T(8,128)(2,1)} reshape(bf16[2,7,128,7,128]{4,3,2,1,0:T(8,128)(2,1)} %copy.56) | data formatting | bytes 6422528 | tf_op jit(solution)/shard_map/reshape | solution.py:102
  248.8 56.7 %all-to-all-done = bf16[32,2,1,2,128,128]{5,4,3,1,2,0:T(8,128)(2,1)} async-done(((bf16[32,2,1,2,128,128]{5,4,3,1,2,0:T(8,128)(2,1)}), bf16[32,2,1,2,128,128]{5,4,3,1,2,0:T(8,128)(2,1)}, u32[]{:S(2)}, u32[]{:S(2)}) %all-to-all-start) | async-done | bytes 4194336 | tf_op jit(solution)/shard_map/all_to_all | solution.py:82
  305.6 4.2 gather_fusion.1
  309.8 4.5 copy.51
  314.3 0.0 copy-start
  314.3 7.6 %reshape.485 = bf16[2,896,896]{2,1,0:T(8,128)(2,1)} reshape(bf16[2,7,128,7,128]{4,3,2,1,0:T(8,128)(2,1)} %copy.51) | data formatting | bytes 6422528 | tf_op jit(solution)/shard_map/reshape | solution.py:102
  321.9 0.0 copy-done
  321.9 23.4 %fusion.2 = f32[2,4096]{1,0:T(2,128)S(1)} fusion(bf16[2,896,896]{2,1,0:T(8,128)(2,1)S(1)} %copy-done, bf16[2,4096,896]{1,2,0:T(8,128)(2,1)} %copy.46, bf16[2,896]{1,0:T(2,128)(2,1)S(1)} %bitcast.68), kind=kOutput, calls=%fused_computation.9 | convolution fusion | flops 13190029312 | bytes 17927680 | tf_op jit(solution)/shard_map/bpi,bij->bpj/dot_general | solution.py:113
  345.3 0.0 copy-start.6
  345.3 24.4 %fusion.1 = f32[2,4096]{1,0:T(2,128)S(1)} fusion(bf16[2,896,896]{2,1,0:T(8,128)(2,1)} %reshape.485, bf16[2,4096,896]{1,2,0:T(8,128)(2,1)} %copy.46, bf16[2,896]{1,0:T(2,128)(2,1)S(1)} %bitcast.69), kind=kOutput, calls=%fused_computation.8 | convolution fusion | flops 13190029312 | bytes 17927680 | tf_op jit(solution)/shard_map/bpi,bij->bpj/dot_general | solution.py:113
  369.8 0.0 copy-done.6
  369.8 0.1 bitcast_select_fusion.1
  369.9 0.0 copy-start.2
  369.9 0.2 broadcast_multiply_fusion
  370.2 0.4 pad.4
  370.5 0.5 copy.69
  371.0 10.5 %fusion = f32[18,1024]{1,0:T(8,128)S(1)} fusion(f32[18,8192]{1,0:T(8,128)S(1)} %bitcast.64, s32[8192]{0:T(1024)S(1)} %bitcast.66), kind=kOutput, calls=%fused_computation.7 | convolution fusion | flops 1820327936 | bytes 696320 | tf_op jit(solution)/shard_map/dot_general | solution.py:123
  381.5 0.0 copy-done.2
  381.5 0.7 reshape.449
  382.2 0.0 all-reduce.3.cloned.1.call-update
  382.2 125.1 %all-reduce.3.cloned.1.call-done = f32[2,9,1024]{2,1,0:T(8,128)} async-done(((f32[2,9,1024]{2,1,0:T(8,128)}), f32[2,9,1024]{2,1,0:T(8,128)}) %all-reduce.3.cloned.1.call-update) | async-done | bytes 73744 | tf_op jit(solution)/shard_map/psum | solution.py:126
  507.3 1.6 copy.59
  (17 shorter events, 0.2 us)
Async XLA Ops:
  207.5 4.3 copy-start.5
  207.5 98.0 %all-to-all-start = ((bf16[32,2,1,2,128,128]{5,4,3,1,2,0:T(8,128)(2,1)}), bf16[32,2,1,2,128,128]{5,4,3,1,2,0:T(8,128)(2,1)}, u32[]{:S(2)}, u32[]{:S(2)}) async-start(bf16[32,2,1,2,128,128]{5,4,3,1,2,0:T(8,128)(2,1)} %get-tuple-element.12), calls=%async_computation | async-start | bytes 8388608 | tf_op jit(solution)/shard_map/all_to_all | solution.py:82
  211.3 295.9 %all-reduce.3.cloned.1.call-start = ((), (), s32[]{:S(2)}) async-start(), calls=%async_computation.2 | async-start | bytes 262144 | tf_op jit(solution)/shard_map/psum | solution.py:126
  212.1 20.0 %copy-start.7 = (s32[2]{0:T(128)S(1)}, s32[2]{0:T(128)}, u32[]{:S(2)}) copy-start(s32[2]{0:T(128)} %param.13) | copy-start | bytes 28
  212.1 20.1 %copy-start.4 = (s32[2,4096]{1,0:T(2,128)S(1)}, s32[2,4096]{1,0:T(2,128)}, u32[]{:S(2)}) copy-start(s32[2,4096]{1,0:T(2,128)} %param.17) | copy-start | bytes 98308
  212.1 20.1 %copy-start.1 = (f32[3,2,4096]{2,1,0:T(2,128)S(1)}, f32[3,2,4096]{2,1,0:T(2,128)}, u32[]{:S(2)}) copy-start(f32[3,2,4096]{2,1,0:T(2,128)} %param.15) | copy-start | bytes 294916
  212.2 20.3 %copy-start.3 = (f32[2,4096]{1,0:T(2,128)S(1)}, f32[2,4096]{1,0:T(2,128)}, u32[]{:S(2)}) copy-start(f32[2,4096]{1,0:T(2,128)} %param.16) | copy-start | bytes 98308
  314.3 7.6 %copy-start = (bf16[2,896,896]{2,1,0:T(8,128)(2,1)S(1)}, bf16[2,896,896]{2,1,0:T(8,128)(2,1)}, u32[]{:S(2)}) copy-start(bf16[2,896,896]{2,1,0:T(8,128)(2,1)} %reshape.487) | copy-start | bytes 9633796
  345.3 24.5 %copy-start.6 = (s32[2]{0:T(128)S(1)}, s32[2]{0:T(128)}, u32[]{:S(2)}) copy-start(s32[2]{0:T(128)} %param.14) | copy-start | bytes 28
  369.9 11.6 %copy-start.2 = (f32[2,2,4096]{2,1,0:T(2,128)}, f32[2,2,4096]{2,1,0:T(2,128)S(1)}, u32[]{:S(2)}) copy-start(f32[2,2,4096]{2,1,0:T(2,128)S(1)} %pad_maximum_fusion) | copy-start | bytes 196612
Sparse Core Ops, SparseCore 0:
  382.3 124.9 all-reduce.2
where the time goes:
time: 525 us; the launch traced here: 516 us
  waiting for transfers between devices  182 us (35%)
  blocking collectives  140 us (27%)
  local copies, waits for them, and re-layouts  110 us (21%)
  matrix products  58.4 us (11%)
  between operations  14.7 us (3%)
  other arithmetic  7.15 us (1%)
    psum x1, waiting for transfers between devices, local(): moments = lax.psum(partial_value, ('row', 'col'))  125 us
    all_to_all x1, blocking collectives, local(): lax.all_to_all(flat_second, ('row', 'col'), split_axis=0, concat_axis=0,...  97.9 us
    all_to_all x1, waiting for transfers between devices, local(): lax.all_to_all(flat_first, ('row', 'col'), split_axis=0, concat_axis=0, t...  56.7 us
    dot_general x2, matrix products, density_of(): jnp.einsum('bpi,bij->bpj', masked, block, preferred_element_type=jnp.floa...  47.8 us
    unnamed x29, local copies, waits for them, and re-layouts  42.4 us
    unnamed x1, blocking collectives  42 us
    reshape x2, local copies, waits for them, and re-layouts, pack_tiles(): stored.reshape(local_rows, tile_size, local_cols, tile_size)  20.1 us
    reshape x2, local copies, waits for them, and re-layouts, assemble(): blocks.transpose(0, 1, 3, 2, 4)  15 us
  transfers between devices with their start and end apart: 2, of which 2 were waited for; matrix products, arithmetic and copies ran while one was open for 7% of the time, Pallas kernels for 0%

commit v1 on v0

v1 whole, which is shorter than its diff:
```python
import functools

import jax
import jax.numpy as jnp
from jax import lax
from jax.experimental import pallas as pl
from jax.experimental.pallas import tpu as pltpu
from jax.sharding import PartitionSpec as P

TILE = 128
ATOMS = 1024
SPREAD = 8
TERMS = 24


def share_kernel(row_count, col_count, mine, every, held, send_sem, recv_sem, self_sem):
    peers = row_count * col_count
    me = lax.axis_index("row") * col_count + lax.axis_index("col")
    barrier = pltpu.get_barrier_semaphore()

    def device(index):
        return (index // col_count, index % col_count)

    def greet(hop, carry):
        pl.semaphore_signal(
            barrier, inc=1, device_id=device((me + hop) % peers),
            device_id_type=pl.DeviceIdType.MESH,
        )
        return carry

    def copy(hop, place):
        return pltpu.make_async_remote_copy(
            src_ref=mine,
            dst_ref=held.at[place],
            send_sem=send_sem.at[hop],
            recv_sem=recv_sem.at[hop],
            device_id=device((me + hop) % peers),
            device_id_type=pl.DeviceIdType.MESH,
        )

    def send(hop, carry):
        copy(hop, me).start()
        return carry

    def finish(hop, carry):
        copy(hop, (me + peers - hop) % peers).wait_recv()
        copy(hop, me).wait_send()
        return carry

    lax.fori_loop(1, peers, greet, 0)
    own = pltpu.make_async_copy(mine, held.at[me], self_sem)
    own.start()
    pl.semaphore_wait(barrier, peers - 1)
    lax.fori_loop(1, peers, send, 0)
    own.wait()
    lax.fori_loop(1, peers, finish, 0)
    every[...] = held[...]


def share(mine, row_count, col_count, collective_id):
    peers = row_count * col_count
    shape = (peers,) + mine.shape
    return pl.pallas_call(
        functools.partial(share_kernel, row_count, col_count),
        out_shape=jax.ShapeDtypeStruct(shape, mine.dtype),
        in_specs=[pl.BlockSpec(memory_space=pltpu.VMEM)],
        out_specs=pl.BlockSpec(memory_space=pltpu.VMEM),
        scratch_shapes=[
            pltpu.VMEM(shape, mine.dtype),
            pltpu.SemaphoreType.DMA((peers,)),
            pltpu.SemaphoreType.DMA((peers,)),
            pltpu.SemaphoreType.DMA,
        ],
        compiler_params=pltpu.CompilerParams(collective_id=collective_id, has_side_effects=True),
        name="share",
    )(mine)


def pack_kernel(row_at, col_at, first, second, out, sem):
    height, width = out.shape[2], out.shape[3]

    def issue(peer, carry):
        rows = pl.ds(pl.multiple_of(row_at[peer] * TILE, TILE), height)
        cols = pl.ds(pl.multiple_of(col_at[peer] * TILE, TILE), width)
        pltpu.make_async_copy(first.at[rows, cols], out.at[peer, 0], sem).start()
        pltpu.make_async_copy(second.at[rows, cols], out.at[peer, 1], sem).start()
        return carry

    lax.fori_loop(0, out.shape[0], issue, 0)
    pltpu.make_async_copy(out, out, sem).wait()


def pack(row_at, col_at, first, second, height, width):
    peers = row_at.shape[0]
    shape = (peers, 2, height, width)
    return pl.pallas_call(
        pack_kernel,
        out_shape=jax.ShapeDtypeStruct(shape, first.dtype),
        in_specs=[
            pl.BlockSpec(memory_space=pltpu.SMEM),
            pl.BlockSpec(memory_space=pltpu.SMEM),
            pl.BlockSpec(memory_space=pl.ANY),
            pl.BlockSpec(memory_space=pl.ANY),
        ],
        out_specs=pl.BlockSpec(memory_space=pltpu.VMEM),
        scratch_shapes=[pltpu.SemaphoreType.DMA],
        cost_estimate=pl.CostEstimate(
            flops=0, bytes_accessed=4 * peers * height * width * 2, transcendentals=0
        ),
        name="pack",
    )(row_at, col_at, first, second)


def density_kernel(
    run, batch, counts, peer_at, row_slot, col_slot, arrived, basis, geometry, atoms,
    density, moments, block, sem,
):
    step = pl.program_id(0)
    points = basis.shape[1]
    span = run * TILE
    live_tiles = counts[0]
    live_points = counts[1]

    @pl.when(step == 0)
    def _():
        def issue(index, carry):
            k = index // run
            l = index % run
            peer = peer_at[index]
            rows = pl.ds(pl.multiple_of(row_slot[k] * TILE, TILE), TILE)
            cols = pl.ds(pl.multiple_of(col_slot[l] * TILE, TILE), TILE)
            to_rows = pl.ds(pl.multiple_of(k * TILE, TILE), TILE)
            for d in range(2):
                to_cols = pl.ds(pl.multiple_of(d * span + l * TILE, TILE), TILE)
                pltpu.make_async_copy(
                    arrived.at[peer, d, rows, cols], block.at[to_rows, to_cols], sem
                ).start()
            return carry

        lax.fori_loop(0, run * run, issue, 0)
        moments[...] = jnp.zeros_like(moments)
        pltpu.make_async_copy(block, block, sem).wait()
        for k in range(run):

            @pl.when(k >= live_tiles)
            def _():
                for l in range(2 * run):
                    block[k * TILE:(k + 1) * TILE, l * TILE:(l + 1) * TILE] = jnp.zeros(
                        (TILE, TILE), block.dtype
                    )
                for d in range(2):
                    for l in range(run):
                        first = d * span + k * TILE
                        block[l * TILE:(l + 1) * TILE, first:first + TILE] = jnp.zeros(
                            (TILE, TILE), block.dtype
                        )

    @pl.when(step * points >= live_points)
    def _():
        density[...] = jnp.zeros_like(density)

    @pl.when(step * points < live_points)
    def _():
        values = basis[0]
        place = step * points + lax.broadcasted_iota(jnp.int32, (1, points), 1)
        live = place < live_points
        rows = []
        for d in range(2):
            product = jnp.dot(
                values, block[:, d * span:(d + 1) * span], preferred_element_type=jnp.float32
            )
            total = None
            for l in range(run):
                part = product[:, l * TILE:(l + 1) * TILE] * values[
                    :, l * TILE:(l + 1) * TILE
                ].astype(jnp.float32)
                total = part if total is None else total + part
            row = jnp.sum(total.T, axis=0, keepdims=True)
            rows.append(jnp.where(live, row, 0.0))
        density[...] = jnp.concatenate(rows, axis=0)
        x = geometry[0:1, :]
        y = geometry[1:2, :]
        z = geometry[2:3, :]
        w = geometry[3:4, :]
        r2 = x * x + y * y + z * z
        weighted = [
            w, w * x, w * y, w * z, w * (x * y), w * (y * z),
            w * (3.0 * z * z - r2), w * (x * z), w * (x * x - y * y),
        ]
        terms = [rows[d] * item for d in range(2) for item in weighted]
        terms += [jnp.zeros((1, points), jnp.float32)] * (TERMS - len(terms))
        stacked = jnp.concatenate(terms, axis=0)
        atom = atoms[...]
        for j in range(SPREAD):
            chosen = jnp.where(atom == j, stacked, 0.0)
            total = None
            for c in range(points // TILE):
                part = chosen[:, c * TILE:(c + 1) * TILE]
                total = part if total is None else total + part
            moments[j] = moments[j] + total


def density_of(batch, counts, peer_at, row_slot, col_slot, arrived, basis, geometry, atoms):
    points, span = basis.shape[1], basis.shape[2]
    run = span // TILE
    chunk = min(512, points)
    grid = points // chunk

    def basis_map(i, counts, *_):
        last = jnp.maximum((counts[1] + chunk - 1) // chunk - 1, 0)
        return (batch, jnp.minimum(i, last), 0)

    return pl.pallas_call(
        functools.partial(density_kernel, run, batch),
        grid_spec=pltpu.PrefetchScalarGridSpec(
            num_scalar_prefetch=4,
            grid=(grid,),
            in_specs=[
                pl.BlockSpec(memory_space=pl.ANY),
                pl.BlockSpec((1, chunk, span), basis_map),
                pl.BlockSpec((4, chunk), lambda i, *_: (0, i)),
                pl.BlockSpec((1, chunk), lambda i, *_: (0, i)),
            ],
            out_specs=[
                pl.BlockSpec((2, chunk), lambda i, *_: (0, i)),
                pl.BlockSpec((SPREAD, TERMS, TILE), lambda i, *_: (0, 0, 0)),
            ],
            scratch_shapes=[
                pltpu.VMEM((span, 2 * span), basis.dtype),
                pltpu.SemaphoreType.DMA,
            ],
        ),
        out_shape=[
            jax.ShapeDtypeStruct((2, points), jnp.float32),
            jax.ShapeDtypeStruct((SPREAD, TERMS, TILE), jnp.float32),
        ],
        compiler_params=pltpu.CompilerParams(
            dimension_semantics=("arbitrary",), vmem_limit_bytes=60 * 1024 * 1024
        ),
        cost_estimate=pl.CostEstimate(
            flops=4 * points * span * span,
            bytes_accessed=2 * points * span + 4 * span * span,
            transcendentals=0,
        ),
        name="density",
    )(counts, peer_at, row_slot, col_slot, arrived, basis, geometry, atoms)


def local(
    density_first,
    density_second,
    basis,
    tile_list,
    tile_count,
    point_count,
    offsets,
    weights,
    atom_of_point,
):
    row_count = lax.axis_size("row")
    col_count = lax.axis_size("col")
    peers = row_count * col_count
    local_rows = density_first.shape[0] // TILE
    local_cols = density_first.shape[1] // TILE
    batches_dev, run = tile_list.shape
    row_slots = min(-(-run // row_count), local_rows)
    col_slots = min(-(-run // col_count), local_cols)
    my_row = lax.axis_index("row")
    my_col = lax.axis_index("col")
    me = my_row * col_count + my_col
    own_start = jnp.min(tile_list, axis=1)
    padded = jnp.pad(own_start[:, None], ((0, -batches_dev % 8), (0, TILE - 1)))
    starts = share(padded, row_count, col_count, 0)[:, :batches_dev, 0]

    def first_held(start, owner, parts, held, slots):
        first = (start + (owner - start) % parts) // parts
        return jnp.minimum(first, held - slots).astype(jnp.int32)

    row_at = first_held(starts, my_row, row_count, local_rows, row_slots)
    col_at = first_held(starts, my_col, col_count, local_cols, col_slots)

    moved = [
        lax.all_to_all(
            pack(
                row_at[:, b], col_at[:, b], density_first, density_second,
                row_slots * TILE, col_slots * TILE,
            ),
            ("row", "col"), split_axis=0, concat_axis=0, tiled=True,
        )
        for b in range(batches_dev)
    ]

    own = own_start[:, None]
    owner_row = tile_list % row_count
    owner_col = tile_list % col_count
    row_slot = tile_list // row_count - first_held(own, owner_row, row_count, local_rows, row_slots)
    col_slot = tile_list // col_count - first_held(own, owner_col, col_count, local_cols, col_slots)
    peer_at = (owner_row[:, :, None] * col_count + owner_col[:, None, :]).reshape(batches_dev, -1)
    stride = ATOMS // (peers * batches_dev)
    base = (me * batches_dev + jnp.arange(batches_dev, dtype=jnp.int32)) * stride
    atom_slot = (atom_of_point - base[:, None]) % ATOMS
    geometry = jnp.concatenate([offsets, weights[None]], axis=0)

    densities = []
    partials = []
    for b in range(batches_dev):
        density, partial = density_of(
            b, jnp.stack([tile_count[b], point_count[b]]), peer_at[b], row_slot[b], col_slot[b],
            moved[b], basis, geometry[:, b], atom_slot[b:b + 1],
        )
        densities.append(density)
        partials.append(jnp.sum(partial, axis=2))
    density = jnp.stack(densities, axis=1)
    mine = jnp.concatenate(partials, axis=0)
    mine = jnp.pad(mine, ((0, 0), (0, TILE - TERMS)))
    every = share(mine, row_count, col_count, 1)
    every = every.reshape(peers * batches_dev, SPREAD, TILE)[:, :, :18]
    blocks = -(-SPREAD // stride)
    every = jnp.pad(every, ((0, 0), (0, blocks * stride - SPREAD), (0, 0)))
    total = None
    for q in range(blocks):
        part = every[:, q * stride:(q + 1) * stride].reshape(ATOMS, 18)
        part = jnp.roll(part, q * stride, axis=0)
        total = part if total is None else total + part
    return density, total.T.reshape(2, 9, ATOMS)


def solution(mesh):
    placed = (
        P("row", "col"),
        P("row", "col"),
        P(("row", "col"), None, None),
        P(("row", "col"), None),
        P(("row", "col")),
        P(("row", "col")),
        P(None, ("row", "col"), None),
        P(("row", "col"), None),
        P(("row", "col"), None),
    )
    return jax.shard_map(
        local,
        mesh=mesh,
        in_specs=placed,
        out_specs=(P(None, ("row", "col"), None), P()),
        check_vma=False,
    )
```

time: 525 us -> 263 us (0.50); the launches traced: 516 us -> 262 us
  blocking collectives: 140 us -> 0 us
  local copies, waits for them, and re-layouts: 110 us -> 8.87 us
  Pallas kernels: 0 us -> 72.3 us
  matrix products: 58.4 us -> 0 us
  waiting for transfers between devices: 182 us -> 160 us
  between operations: 14.7 us -> 0.83 us
  starting transfers between devices: 4.3 us -> 11.4 us
    psum x1 -> x0, waiting for transfers between devices: 125 us -> none  [local(): moments = lax.psum(partial_value, ('row', 'col'))]
    all_to_all x1 -> x2, waiting for transfers between devices: 56.7 us -> 160 us  [local(): lax.all_to_all(pack(row_at[:, b], col_at[:, b], density_first, density_se...]
    all_to_all x1 -> x0, blocking collectives: 97.9 us -> none  [local(): lax.all_to_all(flat_second, ('row', 'col'), split_axis=0, concat_axis=0,...]
    pallas_call x0 -> x6, Pallas kernels: none -> 72.3 us  [the longest x2 36.2 us: density_of(): pl.pallas_call(functools.partial(density_kernel, run, batch), grid_spec=p...]
    dot_general x3 -> x0, matrix products: 58.4 us -> none  [the longest x2 47.8 us: density_of(): jnp.einsum('bpi,bij->bpj', masked, block, preferred_element_type=jnp.floa...]
    unnamed x1 -> x0, blocking collectives: 42 us -> none
    unnamed x29 -> x18, local copies, waits for them, and re-layouts: 42.4 us -> 3.12 us
    reshape x5 -> x2, local copies, waits for them, and re-layouts: 35.8 us -> 0.33 us  [the longest x1 0.32 us: local(): part = every[:, q * stride:(q + 1) * stride].reshape(ATOMS, 18)]
  transfers between devices with their start and end apart: 2 -> 2, of which waited for: 2 -> 2; matrix products, arithmetic and copies ran while one was open for 7% -> 3% of each run, Pallas kernels for 0% -> 7%
where the time goes in v1:
time: 263 us; the launch traced here: 262 us
  waiting for transfers between devices  160 us (61%)
  Pallas kernels  72.3 us (27%)
  starting transfers between devices  11.4 us (4%)
  other arithmetic  8.99 us (3%)
  local copies, waits for them, and re-layouts  8.87 us (3%)
    all_to_all x2, waiting for transfers between devices, local(): lax.all_to_all(pack(row_at[:, b], col_at[:, b], density_first, density_se...  160 us
    pallas_call x2, Pallas kernels, density_of(): pl.pallas_call(functools.partial(density_kernel, run, batch), grid_spec=p...  36.2 us
    pallas_call x2, Pallas kernels, share(): pl.pallas_call(functools.partial(share_kernel, row_count, col_count), out...  25.8 us
    all_to_all x2, starting transfers between devices, local(): lax.all_to_all(pack(row_at[:, b], col_at[:, b], density_first, density_se...  11.4 us
    pallas_call x2, Pallas kernels, pack(): pl.pallas_call(pack_kernel, out_shape=jax.ShapeDtypeStruct(shape, first.d...  10.3 us
  transfers between devices with their start and end apart: 2, of which 2 were waited for; matrix products, arithmetic and copies ran while one was open for 3% of the time, Pallas kernels for 7%

profile of v1, /device:TPU:0, one launch (start us, length us, event | category | flops | bytes accessed | tf_op | source)
XLA Modules:
  0.0 262.4 jit_solution(4292027674300919115)
XLA Ops:
  0.6 0.8 reduce_min.9
  1.4 0.1 copy.21
  1.5 0.6 pad.12.mine
  2.1 12.1 %share.2 = s32[32,8,128]{2,1,0:T(8,128)} custom-call(s32[8,128]{1,0:T(8,128)} %pad.12.mine), custom_call_target="tpu_custom_call" | custom-call | tf_op jit(solution)/shard_map/share/pallas_call | solution.py:63
  14.2 0.9 slice.67
  15.1 0.1 copy.22
  15.3 0.6 slice_bitcast_fusion.4
  15.8 5.1 %pack.2 = bf16[32,2,128,256]{3,2,1,0:T(8,128)(2,1)} custom-call(s32[32]{0:T(128)} %get-tuple-element.45.row_at, s32[32]{0:T(128)} %get-tuple-element.25.col_at, bf16[1536,3072]{1,0:T(8,128)(2,1)} %first.3, bf16[1536,3072]{1,0:T(8,128)(2,1)} %second.3), custom_call_target="tpu_custom_call" | custom-call | bytes 8388608 | tf_op jit(solution)/shard_map/pack/pallas_call | solution.py:96
  21.0 6.2 %all-to-all-start = ((bf16[32,2,128,256]{3,2,1,0:T(8,128)(2,1)}), bf16[32,2,128,256]{3,2,1,0:T(8,128)(2,1)}, u32[]{:S(2)}, u32[]{:S(2)}) async-start(bf16[32,2,128,256]{3,2,1,0:T(8,128)(2,1)} %pack.2), calls=%async_computation | async-start | bytes 8388608 | tf_op jit(solution)/shard_map/all_to_all | solution.py:283
  27.1 5.1 %pack.3 = bf16[32,2,128,256]{3,2,1,0:T(8,128)(2,1)} custom-call(s32[32]{0:T(128)} %get-tuple-element.44.row_at, s32[32]{0:T(128)} %get-tuple-element.26.col_at, bf16[1536,3072]{1,0:T(8,128)(2,1)} %first.3, bf16[1536,3072]{1,0:T(8,128)(2,1)} %second.3), custom_call_target="tpu_custom_call" | custom-call | bytes 8388608 | tf_op jit(solution)/shard_map/pack/pallas_call | solution.py:96
  32.3 0.0 copy-start.4
  32.3 0.0 copy-start
  32.3 0.0 copy-start.1
  32.3 0.0 copy-start.5
  32.3 0.0 copy-start.6
  32.3 0.0 copy-start.2
  32.4 89.0 %all-to-all-done.arrived = bf16[32,2,128,256]{3,2,1,0:T(8,128)(2,1)} async-done(((bf16[32,2,128,256]{3,2,1,0:T(8,128)(2,1)}), bf16[32,2,128,256]{3,2,1,0:T(8,128)(2,1)}, u32[]{:S(2)}, u32[]{:S(2)}) %all-to-all-start) | async-done | bytes 4194336 | tf_op jit(solution)/shard_map/all_to_all | solution.py:283
  121.4 5.2 %all-to-all-start.1 = ((bf16[32,2,128,256]{3,2,1,0:T(8,128)(2,1)}), bf16[32,2,128,256]{3,2,1,0:T(8,128)(2,1)}, u32[]{:S(2)}, u32[]{:S(2)}) async-start(bf16[32,2,128,256]{3,2,1,0:T(8,128)(2,1)} %pack.3), calls=%async_computation.1 | async-start | bytes 8388608 | tf_op jit(solution)/shard_map/all_to_all | solution.py:283
  126.6 0.0 copy-done.4
  126.6 0.1 fusion.8
  126.7 0.1 broadcast_add_fusion
  126.7 0.6 squeeze.39.peer_at
  127.4 0.0 copy-done
  127.4 0.1 copy.23
  127.4 0.0 copy-done.1
  127.5 0.6 squeeze.46.peer_at
  128.1 0.0 copy-done.5
  128.1 0.0 copy-done.6
  128.1 0.6 fusion.18
  128.7 1.9 pad_add_fusion.counts
  130.6 1.9 pad_add_fusion.1.counts
  132.5 0.6 slice_bitcast_fusion.6
  133.1 0.7 fusion.1
  133.8 0.0 copy-done.2
  133.8 0.1 and_select_fusion
  134.0 0.6 fusion.16
  134.6 14.1 %density.2 = (f32[2,4096]{1,0:T(2,128)}, f32[8,24,128]{2,1,0:T(8,128)}) custom-call(s32[2]{0:T(128)} %pad_add_fusion.counts, s32[49]{0:T(128)} %squeeze.39.peer_at, s32[7]{0:T(128)} %get-tuple-element.43.row_slot, s32[7]{0:T(128)} %get-tuple-element.29.col_slot, bf16[32,2,128,256]{3,2,1,0:T(8,128)(2,1)} %all-to-all-done.arrived, ...), custom_call_target="tpu_custom_call" | custom-call | flops 13153337344 | bytes 10551296 | tf_op jit(solution)/shard_map/density/pallas_call | solution.py:213
  148.7 1.0 reduce_sum.18
  149.7 71.1 %all-to-all-done.1.arrived = bf16[32,2,128,256]{3,2,1,0:T(8,128)(2,1)} async-done(((bf16[32,2,128,256]{3,2,1,0:T(8,128)(2,1)}), bf16[32,2,128,256]{3,2,1,0:T(8,128)(2,1)}, u32[]{:S(2)}, u32[]{:S(2)}) %all-to-all-start.1) | async-done | bytes 4194336 | tf_op jit(solution)/shard_map/all_to_all | solution.py:283
  220.8 0.0 copy-start.3
  220.8 22.0 %density.3 = (f32[2,4096]{1,0:T(2,128)}, f32[8,24,128]{2,1,0:T(8,128)}) custom-call(s32[2]{0:T(128)} %pad_add_fusion.1.counts, s32[49]{0:T(128)} %squeeze.46.peer_at, s32[7]{0:T(128)} %get-tuple-element.42.row_slot, s32[7]{0:T(128)} %get-tuple-element.30.col_slot, bf16[32,2,128,256]{3,2,1,0:T(8,128)(2,1)} %all-to-all-done.1.arrived, ...), custom_call_target="tpu_custom_call" | custom-call | flops 13153337344 | bytes 10551296 | tf_op jit(solution)/shard_map/density/pallas_call | solution.py:213
  242.9 1.0 reduce_sum.19
  243.9 0.6 select_maximum_fusion.mine
  244.5 13.7 %share.3 = f32[32,16,128]{2,1,0:T(8,128)} custom-call(f32[16,128]{1,0:T(8,128)} %select_maximum_fusion.mine), custom_call_target="tpu_custom_call" | custom-call | tf_op jit(solution)/shard_map/share/pallas_call | solution.py:63
  258.2 1.6 copy.27
  259.9 0.1 pad.14
  259.9 0.3 reshape.28
  260.3 0.7 copy.26
  260.9 0.0 copy-done.3
  261.0 0.8 pad_maximum_fusion.1
  261.7 0.7 copy.25
  (5 shorter events, 0.1 us)
Async XLA Ops:
  21.0 100.4 %all-to-all-start = ((bf16[32,2,128,256]{3,2,1,0:T(8,128)(2,1)}), bf16[32,2,128,256]{3,2,1,0:T(8,128)(2,1)}, u32[]{:S(2)}, u32[]{:S(2)}) async-start(bf16[32,2,128,256]{3,2,1,0:T(8,128)(2,1)} %pack.2), calls=%async_computation | async-start | bytes 8388608 | tf_op jit(solution)/shard_map/all_to_all | solution.py:283
  32.3 94.3 %copy-start.4 = (s32[2,7]{1,0:T(2,128)S(1)}, s32[2,7]{1,0:T(2,128)}, u32[]{:S(2)}) copy-start(s32[2,7]{1,0:T(2,128)} %param.12) | copy-start | bytes 172
  32.3 95.1 %copy-start = (f32[3,2,4096]{2,1,0:T(2,128)S(1)}, f32[3,2,4096]{2,1,0:T(2,128)}, u32[]{:S(2)}) copy-start(f32[3,2,4096]{2,1,0:T(2,128)} %param.15) | copy-start | bytes 294916
  32.3 95.1 %copy-start.1 = (f32[2,4096]{1,0:T(2,128)S(1)}, f32[2,4096]{1,0:T(2,128)}, u32[]{:S(2)}) copy-start(f32[2,4096]{1,0:T(2,128)} %param.16) | copy-start | bytes 98308
  32.3 95.8 %copy-start.5 = (s32[2]{0:T(128)S(1)}, s32[2]{0:T(128)}, u32[]{:S(2)}) copy-start(s32[2]{0:T(128)} %param.13) | copy-start | bytes 28
  32.3 95.8 %copy-start.6 = (s32[2]{0:T(128)S(1)}, s32[2]{0:T(128)}, u32[]{:S(2)}) copy-start(s32[2]{0:T(128)} %param.14) | copy-start | bytes 28
  32.3 101.5 %copy-start.2 = (s32[2,4096]{1,0:T(2,128)S(1)}, s32[2,4096]{1,0:T(2,128)}, u32[]{:S(2)}) copy-start(s32[2,4096]{1,0:T(2,128)} %param.17) | copy-start | bytes 98308
  121.4 99.4 %all-to-all-start.1 = ((bf16[32,2,128,256]{3,2,1,0:T(8,128)(2,1)}), bf16[32,2,128,256]{3,2,1,0:T(8,128)(2,1)}, u32[]{:S(2)}, u32[]{:S(2)}) async-start(bf16[32,2,128,256]{3,2,1,0:T(8,128)(2,1)} %pack.3), calls=%async_computation.1 | async-start | bytes 8388608 | tf_op jit(solution)/shard_map/all_to_all | solution.py:283
  220.8 40.1 %copy-start.3 = (f32[2,4096]{1,0:T(2,128)S(1)}, f32[2,4096]{1,0:T(2,128)}, u32[]{:S(2)}) copy-start(f32[2,4096]{1,0:T(2,128)} %get-tuple-element.6) | copy-start | bytes 98308

commit v2 on v1

--- a/solution.py
+++ b/solution.py
@@ -161,23 +161,32 @@
 
     @pl.when(step * points < live_points)
     def _():
-        values = basis[0]
         place = step * points + lax.broadcasted_iota(jnp.int32, (1, points), 1)
         live = place < live_points
-        rows = []
-        for d in range(2):
-            product = jnp.dot(
-                values, block[:, d * span:(d + 1) * span], preferred_element_type=jnp.float32
-            )
-            total = None
-            for l in range(run):
-                part = product[:, l * TILE:(l + 1) * TILE] * values[
-                    :, l * TILE:(l + 1) * TILE
-                ].astype(jnp.float32)
-                total = part if total is None else total + part
-            row = jnp.sum(total.T, axis=0, keepdims=True)
-            rows.append(jnp.where(live, row, 0.0))
-        density[...] = jnp.concatenate(rows, axis=0)
+        fewest = max(run - 2, 1)
+        for used in range(fewest, run + 1):
+            width = used * TILE
+
+            @pl.when(live_tiles <= used if used == fewest else live_tiles == used)
+            def _():
+                values = basis[0, :, 0:width]
+                parts = []
+                for d in range(2):
+                    product = jnp.dot(
+                        values, block[0:width, d * span:d * span + width],
+                        preferred_element_type=jnp.float32,
+                    )
+                    total = None
+                    for l in range(used):
+                        part = product[:, l * TILE:(l + 1) * TILE] * values[
+                            :, l * TILE:(l + 1) * TILE
+                        ].astype(jnp.float32)
+                        total = part if total is None else total + part
+                    row = jnp.sum(total.T, axis=0, keepdims=True)
+                    parts.append(jnp.where(live, row, 0.0))
+                density[...] = jnp.concatenate(parts, axis=0)
+
+        rows = [density[d:d + 1, :] for d in range(2)]
         x = geometry[0:1, :]
         y = geometry[1:2, :]
         z = geometry[2:3, :]
@@ -269,8 +278,8 @@
     my_col = lax.axis_index("col")
     me = my_row * col_count + my_col
     own_start = jnp.min(tile_list, axis=1)
-    padded = jnp.pad(own_start[:, None], ((0, -batches_dev % 8), (0, TILE - 1)))
-    starts = share(padded, row_count, col_count, 0)[:, :batches_dev, 0]
+    padded = jnp.pad(own_start[None, :], ((0, 0), (0, TILE - batches_dev)))
+    starts = share(padded, row_count, col_count, 0)[:, 0, :batches_dev]
 
     def first_held(start, owner, parts, held, slots):
         first = (start + (owner - start) % parts) // parts
@@ -311,10 +320,12 @@
         densities.append(density)
         partials.append(jnp.sum(partial, axis=2))
     density = jnp.stack(densities, axis=1)
-    mine = jnp.concatenate(partials, axis=0)
-    mine = jnp.pad(mine, ((0, 0), (0, TILE - TERMS)))
+    mine = jnp.concatenate(partials, axis=1)
+    mine = jnp.pad(mine, ((0, 0), (0, -mine.shape[1] % TILE)))
     every = share(mine, row_count, col_count, 1)
-    every = every.reshape(peers * batches_dev, SPREAD, TILE)[:, :, :18]
+    every = jnp.stack(
+        [every[:, :, b * TERMS:b * TERMS + 18] for b in range(batches_dev)], axis=1
+    ).reshape(peers * batches_dev, SPREAD, 18)
     blocks = -(-SPREAD // stride)
     every = jnp.pad(every, ((0, 0), (0, blocks * stride - SPREAD), (0, 0)))
     total = None

time: 263 us -> 258 us (0.981)
  waiting for transfers between devices: 160 us -> 157 us
    pallas_call x2, Pallas kernels: 25.8 us -> 33.1 us  [share(): pl.pallas_call(functools.partial(share_kernel, row_count, col_count), out...]
    pallas_call x2, Pallas kernels: 36.2 us -> 30 us  [density_of(): pl.pallas_call(functools.partial(density_kernel, run, batch), grid_spec=p...]
    all_to_all x2, waiting for transfers between devices: 160 us -> 157 us  [local(): lax.all_to_all(pack(row_at[:, b], col_at[:, b], density_first, density_se...]
  transfers between devices with their start and end apart: 2 -> 2, of which waited for: 2 -> 2; matrix products, arithmetic and copies ran while one was open for 3% -> 3% of each run, Pallas kernels for 7% -> 9%
where the time goes in v2:
time: 258 us
  waiting for transfers between devices  157 us (61%)
  Pallas kernels  73.5 us (28%)
  starting transfers between devices  10.4 us (4%)
  other arithmetic  9 us (3%)
  local copies, waits for them, and re-layouts  7.73 us (3%)
    all_to_all x2, waiting for transfers between devices, local(): lax.all_to_all(pack(row_at[:, b], col_at[:, b], density_first, density_se...  157 us
    pallas_call x2, Pallas kernels, share(): pl.pallas_call(functools.partial(share_kernel, row_count, col_count), out...  33.1 us
    pallas_call x2, Pallas kernels, density_of(): pl.pallas_call(functools.partial(density_kernel, run, batch), grid_spec=p...  30 us
    pallas_call x2, Pallas kernels, pack(): pl.pallas_call(pack_kernel, out_shape=jax.ShapeDtypeStruct(shape, first.d...  10.5 us
    all_to_all x2, starting transfers between devices, local(): lax.all_to_all(pack(row_at[:, b], col_at[:, b], density_first, density_se...  10.4 us
  transfers between devices with their start and end apart: 2, of which 2 were waited for; matrix products, arithmetic and copies ran while one was open for 3% of the time, Pallas kernels for 9%

profile of v2, /device:TPU:0, one launch (start us, length us, event | category | flops | bytes accessed | tf_op | source)
XLA Modules:
  0.0 258.3 jit_solution(4435170023396338899)
XLA Ops:
  0.6 0.8 reduce_min.9
  1.4 0.5 pad.12.mine
  2.0 11.4 %share.2 = s32[32,1,128]{2,1,0:T(1,128)} custom-call(s32[1,128]{1,0:T(1,128)} %pad.12.mine), custom_call_target="tpu_custom_call" | custom-call | tf_op jit(solution)/shard_map/share/pallas_call | solution.py:63
  13.4 0.8 copy.14
  14.2 0.5 slice_bitcast_fusion.6
  14.7 5.2 %pack.2 = bf16[32,2,128,256]{3,2,1,0:T(8,128)(2,1)} custom-call(s32[32]{0:T(128)} %get-tuple-element.45.row_at, s32[32]{0:T(128)} %get-tuple-element.25.col_at, bf16[1536,3072]{1,0:T(8,128)(2,1)} %first.3, bf16[1536,3072]{1,0:T(8,128)(2,1)} %second.3), custom_call_target="tpu_custom_call" | custom-call | bytes 8388608 | tf_op jit(solution)/shard_map/pack/pallas_call | solution.py:96
  19.9 5.2 %all-to-all-start = ((bf16[32,2,128,256]{3,2,1,0:T(8,128)(2,1)}), bf16[32,2,128,256]{3,2,1,0:T(8,128)(2,1)}, u32[]{:S(2)}, u32[]{:S(2)}) async-start(bf16[32,2,128,256]{3,2,1,0:T(8,128)(2,1)} %pack.2), calls=%async_computation | async-start | bytes 8388608 | tf_op jit(solution)/shard_map/all_to_all | solution.py:292
  25.2 5.3 %pack.3 = bf16[32,2,128,256]{3,2,1,0:T(8,128)(2,1)} custom-call(s32[32]{0:T(128)} %get-tuple-element.44.row_at, s32[32]{0:T(128)} %get-tuple-element.26.col_at, bf16[1536,3072]{1,0:T(8,128)(2,1)} %first.3, bf16[1536,3072]{1,0:T(8,128)(2,1)} %second.3), custom_call_target="tpu_custom_call" | custom-call | bytes 8388608 | tf_op jit(solution)/shard_map/pack/pallas_call | solution.py:96
  30.4 0.0 copy-start.4
  30.4 0.0 copy-start
  30.4 0.0 copy-start.1
  30.5 0.0 copy-start.5
  30.5 0.0 copy-start.6
  30.5 0.0 copy-start.2
  30.5 88.9 %all-to-all-done.arrived = bf16[32,2,128,256]{3,2,1,0:T(8,128)(2,1)} async-done(((bf16[32,2,128,256]{3,2,1,0:T(8,128)(2,1)}), bf16[32,2,128,256]{3,2,1,0:T(8,128)(2,1)}, u32[]{:S(2)}, u32[]{:S(2)}) %all-to-all-start) | async-done | bytes 4194336 | tf_op jit(solution)/shard_map/all_to_all | solution.py:292
  119.4 5.2 %all-to-all-start.1 = ((bf16[32,2,128,256]{3,2,1,0:T(8,128)(2,1)}), bf16[32,2,128,256]{3,2,1,0:T(8,128)(2,1)}, u32[]{:S(2)}, u32[]{:S(2)}) async-start(bf16[32,2,128,256]{3,2,1,0:T(8,128)(2,1)} %pack.3), calls=%async_computation.1 | async-start | bytes 8388608 | tf_op jit(solution)/shard_map/all_to_all | solution.py:292
  124.6 0.0 copy-done.4
  124.6 0.1 fusion.8
  124.7 0.1 broadcast_add_fusion
  124.8 0.6 squeeze.39.peer_at
  125.4 0.0 copy-done
  125.4 0.1 copy.15
  125.4 0.0 copy-done.1
  125.5 0.7 squeeze.46.peer_at
  126.1 0.0 copy-done.5
  126.1 0.0 copy-done.6
  126.1 0.6 fusion.18
  126.7 1.9 pad_add_fusion.counts
  128.6 1.8 pad_add_fusion.1.counts
  130.5 0.6 slice_bitcast_fusion.8
  131.0 0.7 fusion.1
  131.7 0.0 copy-done.2
  131.7 0.1 and_select_fusion
  131.9 0.6 fusion.16
  132.5 17.5 %density.2 = (f32[2,4096]{1,0:T(2,128)}, f32[8,24,128]{2,1,0:T(8,128)}) custom-call(s32[2]{0:T(128)} %pad_add_fusion.counts, s32[49]{0:T(128)} %squeeze.39.peer_at, s32[7]{0:T(128)} %get-tuple-element.43.row_slot, s32[7]{0:T(128)} %get-tuple-element.29.col_slot, bf16[32,2,128,256]{3,2,1,0:T(8,128)(2,1)} %all-to-all-done.arrived, ...), custom_call_target="tpu_custom_call" | custom-call | flops 13153337344 | bytes 10551296 | tf_op jit(solution)/shard_map/density/pallas_call | solution.py:222
  150.0 1.0 reduce_sum.18
  151.0 67.8 %all-to-all-done.1.arrived = bf16[32,2,128,256]{3,2,1,0:T(8,128)(2,1)} async-done(((bf16[32,2,128,256]{3,2,1,0:T(8,128)(2,1)}), bf16[32,2,128,256]{3,2,1,0:T(8,128)(2,1)}, u32[]{:S(2)}, u32[]{:S(2)}) %all-to-all-start.1) | async-done | bytes 4194336 | tf_op jit(solution)/shard_map/all_to_all | solution.py:292
  218.8 0.0 copy-start.3
  218.8 12.5 %density.3 = (f32[2,4096]{1,0:T(2,128)}, f32[8,24,128]{2,1,0:T(8,128)}) custom-call(s32[2]{0:T(128)} %pad_add_fusion.1.counts, s32[49]{0:T(128)} %squeeze.46.peer_at, s32[7]{0:T(128)} %get-tuple-element.42.row_slot, s32[7]{0:T(128)} %get-tuple-element.30.col_slot, bf16[32,2,128,256]{3,2,1,0:T(8,128)(2,1)} %all-to-all-done.1.arrived, ...), custom_call_target="tpu_custom_call" | custom-call | flops 13153337344 | bytes 10551296 | tf_op jit(solution)/shard_map/density/pallas_call | solution.py:222
  231.3 1.0 reduce_sum.19
  232.3 0.7 select_maximum_fusion.mine
  233.0 21.7 %share.3 = f32[32,8,128]{2,1,0:T(8,128)} custom-call(f32[8,128]{1,0:T(8,128)} %select_maximum_fusion.mine), custom_call_target="tpu_custom_call" | custom-call | tf_op jit(solution)/shard_map/share/pallas_call | solution.py:63
  254.7 1.1 slice_bitcast_fusion.1
  255.9 0.2 copy.17
  256.1 0.7 copy.19
  256.8 0.0 copy-done.3
  256.8 0.8 pad_maximum_fusion.2
  257.6 0.7 copy.18
  (8 shorter events, 0.2 us)
Async XLA Ops:
  19.9 99.5 %all-to-all-start = ((bf16[32,2,128,256]{3,2,1,0:T(8,128)(2,1)}), bf16[32,2,128,256]{3,2,1,0:T(8,128)(2,1)}, u32[]{:S(2)}, u32[]{:S(2)}) async-start(bf16[32,2,128,256]{3,2,1,0:T(8,128)(2,1)} %pack.2), calls=%async_computation | async-start | bytes 8388608 | tf_op jit(solution)/shard_map/all_to_all | solution.py:292
  30.4 94.2 %copy-start.4 = (s32[2,7]{1,0:T(2,128)S(1)}, s32[2,7]{1,0:T(2,128)}, u32[]{:S(2)}) copy-start(s32[2,7]{1,0:T(2,128)} %param.12) | copy-start | bytes 172
  30.4 94.9 %copy-start = (f32[3,2,4096]{2,1,0:T(2,128)S(1)}, f32[3,2,4096]{2,1,0:T(2,128)}, u32[]{:S(2)}) copy-start(f32[3,2,4096]{2,1,0:T(2,128)} %param.15) | copy-start | bytes 294916
  30.4 95.0 %copy-start.1 = (f32[2,4096]{1,0:T(2,128)S(1)}, f32[2,4096]{1,0:T(2,128)}, u32[]{:S(2)}) copy-start(f32[2,4096]{1,0:T(2,128)} %param.16) | copy-start | bytes 98308
  30.5 95.7 %copy-start.5 = (s32[2]{0:T(128)S(1)}, s32[2]{0:T(128)}, u32[]{:S(2)}) copy-start(s32[2]{0:T(128)} %param.13) | copy-start | bytes 28
  30.5 95.7 %copy-start.6 = (s32[2]{0:T(128)S(1)}, s32[2]{0:T(128)}, u32[]{:S(2)}) copy-start(s32[2]{0:T(128)} %param.14) | copy-start | bytes 28
  30.5 101.3 %copy-start.2 = (s32[2,4096]{1,0:T(2,128)S(1)}, s32[2,4096]{1,0:T(2,128)}, u32[]{:S(2)}) copy-start(s32[2,4096]{1,0:T(2,128)} %param.17) | copy-start | bytes 98308
  119.4 99.4 %all-to-all-start.1 = ((bf16[32,2,128,256]{3,2,1,0:T(8,128)(2,1)}), bf16[32,2,128,256]{3,2,1,0:T(8,128)(2,1)}, u32[]{:S(2)}, u32[]{:S(2)}) async-start(bf16[32,2,128,256]{3,2,1,0:T(8,128)(2,1)} %pack.3), calls=%async_computation.1 | async-start | bytes 8388608 | tf_op jit(solution)/shard_map/all_to_all | solution.py:292
  218.8 38.0 %copy-start.3 = (f32[2,4096]{1,0:T(2,128)S(1)}, f32[2,4096]{1,0:T(2,128)}, u32[]{:S(2)}) copy-start(f32[2,4096]{1,0:T(2,128)} %get-tuple-element.6) | copy-start | bytes 98308
